TPU v7x, 256 devices: a whole 4x4x8 slice. The times are simulated.
256 devices in a mesh: grp: 16 (over z, core), sub: 16 (over x, y).
Axes of the slice: x: 4, y: 4, z: 8, core: 2. Of those that a mesh axis runs over, the one named last changes fastest.
Arguments:
- coarse_op: float32 [256, 64, 576], P(('grp', 'sub'))
- right_side: float32 [256, 64, 64], P(('grp', 'sub')), may hold values from -6 to 6
- owner_map: int32 [256], replicated, may hold values from 0 to 255, as said below
- neighbor_table: int32 [256, 8], replicated, may hold values from 0 to 255, as said below
Outputs:
- solution: float32 [256, 64, 64], P(('grp', 'sub'))
Inputs may be any that keep to these rules, and one draw needn't show every extreme that they name: `owner_map`: a permutation of 0 .. 255. `neighbor_table`: row t lists the neighbours of coarse site t on a periodic 4^4 lattice in the order +x, -x, +y, -y, +z, -z, +t, -t; lattice positions carry the site numbers in a permuted order.
All inputs are finite; a program needn't handle non-finite values.
Results may differ from a plain program's by a relative error of at most 0.0001.
Values sent between devices are 32-bit elements; how exact they have to be, the bound alone decides.
A program may use at most 64 MiB of HBM per device.

v0:
```python
import jax
import jax.numpy as jnp
from jax import lax
from jax.sharding import PartitionSpec as P

ITERS = 3


def from_everyone(array, axis):
    copies = jnp.broadcast_to(array, (lax.axis_size(axis), *array.shape))
    return lax.all_to_all(copies, axis, split_axis=0, concat_axis=0, tiled=True)


def laid_out(parts, dim):
    parts = jnp.moveaxis(parts, 0, dim)
    shape = parts.shape
    return parts.reshape(*shape[:dim], shape[dim] * shape[dim + 1], *shape[dim + 2 :])


def gathered_copies(array, axis, dim):
    parts = from_everyone(array, axis)
    return laid_out(parts, dim)


def over_copies(array, axis):
    return from_everyone(array, axis).sum(axis=0)


def inner_product(first, second):
    return jnp.sum(first * second, axis=(0, 1))


def per_device(coarse_op, right_side, owner_map, neighbor_table):
    n_sub = lax.axis_size("sub")
    n_grp = lax.axis_size("grp")
    per_dev = coarse_op.shape[0]
    dof_count = coarse_op.shape[1]
    site_count = owner_map.shape[0]
    site_ids = jnp.arange(site_count, dtype=jnp.int32)
    inverse = jnp.sum(
        jnp.where(owner_map[None, :] == site_ids[:, None], site_ids[None, :], 0), axis=1
    )
    link = inverse[neighbor_table[owner_map]]
    op_rows = lax.all_gather(coarse_op, "grp", axis=0, tiled=True)
    rhs_rows = lax.all_to_all(right_side, "grp", split_axis=2, concat_axis=0, tiled=True)

    def reduce_sum(values):
        return jax.tree.map(lambda part: over_copies(part, "sub"), values)

    row_count = op_rows.shape[0]
    local_rows = jnp.arange(row_count, dtype=jnp.int32)
    own_slots = (
        local_rows // per_dev * n_sub + lax.axis_index("sub")
    ) * per_dev + local_rows % per_dev
    target = link[own_slots]
    target_block = target // per_dev
    position = (target_block % n_sub * n_grp + target_block // n_sub) * per_dev + target % per_dev
    rhs_count = rhs_rows.shape[2]
    beta = jnp.sqrt(reduce_sum(inner_product(rhs_rows, rhs_rows)))
    krylov = [rhs_rows / beta]
    hess = jnp.zeros((ITERS + 1, ITERS, rhs_count), jnp.float32)
    for column in range(ITERS):
        apply_vector = krylov[column]
        piece = gathered_copies(apply_vector, "sub", 0)
        count = piece.shape[0]
        select = (position[:, :, None] == jnp.arange(count, dtype=jnp.int32)[None, None, :]).astype(
            jnp.float32
        )
        nearby = jnp.einsum("lkr,rab->lkab", select, piece, precision=lax.Precision.HIGHEST)
        stacked = jnp.concatenate([apply_vector[:, None], nearby], axis=1).reshape(
            row_count, 9 * dof_count, rhs_count
        )
        image = jnp.einsum("sac,scr->sar", op_rows, stacked, precision=lax.Precision.HIGHEST)
        totals = reduce_sum(
            tuple(
                [inner_product(vector, image) for vector in krylov] + [inner_product(image, image)]
            )
        )
        norm_sq = totals[-1]
        for index_i in range(column + 1):
            image = image - totals[index_i] * krylov[index_i]
            hess = hess.at[index_i, column].set(totals[index_i])
            norm_sq = norm_sq - totals[index_i] * totals[index_i]
        norm_value = jnp.sqrt(norm_sq)
        hess = hess.at[column + 1, column].set(norm_value)
        krylov.append(image / norm_value)
    gram_matrix = jnp.einsum("ijr,ikr->rjk", hess, hess, precision=lax.Precision.HIGHEST)
    projected = (beta[None, :] * hess[0]).T
    factor = jnp.linalg.cholesky(gram_matrix)
    halfway = jax.scipy.linalg.solve_triangular(factor, projected[..., None], lower=True)
    weights = jax.scipy.linalg.solve_triangular(factor, halfway, lower=True, trans=1)[..., 0]
    solution = jnp.zeros_like(rhs_rows)
    for column in range(ITERS):
        solution = solution + weights[:, column][None, None, :] * krylov[column]
    return lax.all_to_all(solution, "grp", split_axis=0, concat_axis=2, tiled=True)


def solution(mesh):
    placed = (P(("grp", "sub"), None, None), P(("grp", "sub"), None, None), P(), P())
    return jax.shard_map(
        per_device,
        mesh=mesh,
        in_specs=placed,
        out_specs=P(("grp", "sub"), None, None),
        check_vma=False,
    )
```

profile of v0, /device:TPU:1, one launch (start us, length us, event | category | flops | bytes accessed | tf_op | source)
XLA Modules:
  0.0 240.6 jit_solution(6348703550296950979)
XLA Ops:
  10.1 10.0 %all-to-all-start = ((f32[16,1,256]{2,1,0:T(1,128)}), f32[16,1,256]{2,1,0:T(1,128)S(1)}, u32[]{:S(2)}, u32[]{:S(2)}) async-start(f32[16,1,256]{2,1,0:T(1,128)} %reshape.567), calls=%async_computation | async-start | bytes 32768 | tf_op jit(solution)/shard_map/all_to_all | solution.py:45
  23.3 4.1 %all-to-all-done = f32[16,1,256]{2,1,0:T(1,128)S(1)} async-done(((f32[16,1,256]{2,1,0:T(1,128)}), f32[16,1,256]{2,1,0:T(1,128)S(1)}, u32[]{:S(2)}, u32[]{:S(2)}) %all-to-all-start) | async-done | bytes 16416 | tf_op jit(solution)/shard_map/all_to_all | solution.py:45
  29.0 6.8 %all-to-all-start.1 = ((f32[16,1,4]{2,1,0:T(1,128)}), f32[16,1,4]{2,1,0:T(1,128)S(1)}, u32[]{:S(2)}, u32[]{:S(2)}) async-start(f32[16,1,4]{2,1,0:T(1,128)} %broadcast_in_dim.48), calls=%async_computation.1 | async-start | bytes 16384 | tf_op jit(solution)/shard_map/all_to_all | solution.py:11
  35.8 13.1 %gather_fusion.1 = s32[2048]{0:T(1024)S(1)} fusion(s32[256]{0:T(256)S(1)} %select_reduce_fusion, s32[2048]{0:T(1024)S(1)} %broadcast_clamp_fusion), kind=kCustom, calls=%fused_computation.1 | custom fusion | bytes 24576 | tf_op jit(solution)/shard_map/gather | solution.py:43
  50.8 6.7 %all-to-all-start.2 = ((f32[16,1,4096]{2,1,0:T(1,128)}), f32[16,1,4096]{2,1,0:T(1,128)S(1)}, u32[]{:S(2)}, u32[]{:S(2)}) async-start(f32[16,1,4096]{2,1,0:T(1,128)} %reshape.569), calls=%async_computation.2 | async-start | bytes 524288 | tf_op jit(solution)/shard_map/all_to_all | solution.py:11
  57.6 7.3 %all-to-all-done.2 = f32[16,1,4096]{2,1,0:T(1,128)S(1)} async-done(((f32[16,1,4096]{2,1,0:T(1,128)}), f32[16,1,4096]{2,1,0:T(1,128)S(1)}, u32[]{:S(2)}, u32[]{:S(2)}) %all-to-all-start.2) | async-done | bytes 262176 | tf_op jit(solution)/shard_map/all_to_all | solution.py:11
  67.1 4.5 %multiply_reduce_fusion.8 = (f32[4]{0:T(128)S(1)}, f32[4]{0:T(128)S(1)}, f32[16,64,4]{1,2,0:T(4,128)S(1)}) fusion(f32[16,64,4]{1,2,0:T(4,128)S(1)} %broadcast_divide_fusion.1, f32[16,576,4]{1,2,0:T(4,128)S(1)} %reshape.564, f32[16,64,576]{2,1,0:T(8,128)} %all-gather.2.cloned.1.call-done), kind=kOutput, calls=%fused_computation.31 | convolution fusion | flops 28327928 | bytes 2539552 | tf_op jit(solution)/shard_map/sac,scr->sar/dot_general | solution.py:73
  71.6 9.8 %all_to_all.111 = f32[16,1,4]{2,1,0:T(1,128)S(1)} all-to-all(f32[16,1,4]{2,1,0:T(1,128)S(1)} %broadcast_in_dim.90), channel_id=1, replica_groups=mesh['grp'=16,'sub'=16] {'sub'}, dimensions={0} | all-to-all | bytes 512 | tf_op jit(solution)/shard_map/all_to_all | solution.py:11
  82.0 3.5 %all-to-all-start.4 = ((f32[16,1,4]{2,1,0:T(1,128)}), f32[16,1,4]{2,1,0:T(1,128)S(1)}, u32[]{:S(2)}, u32[]{:S(2)}) async-start(f32[16,1,4]{2,1,0:T(1,128)} %broadcast_in_dim.91), calls=%async_computation.4 | async-start | bytes 16384 | tf_op jit(solution)/shard_map/all_to_all | solution.py:11
  85.6 6.3 %all-to-all-done.4 = f32[16,1,4]{2,1,0:T(1,128)S(1)} async-done(((f32[16,1,4]{2,1,0:T(1,128)}), f32[16,1,4]{2,1,0:T(1,128)S(1)}, u32[]{:S(2)}, u32[]{:S(2)}) %all-to-all-start.4) | async-done | bytes 288 | tf_op jit(solution)/shard_map/all_to_all | solution.py:11
  93.0 3.8 %all-to-all-start.5 = ((f32[16,1,4096]{2,1,0:T(1,128)}), f32[16,1,4096]{2,1,0:T(1,128)S(1)}, u32[]{:S(2)}, u32[]{:S(2)}) async-start(f32[16,1,4096]{2,1,0:T(1,128)} %reshape.571), calls=%async_computation.5 | async-start | bytes 524288 | tf_op jit(solution)/shard_map/all_to_all | solution.py:11
  97.6 6.6 %all-to-all-done.5 = f32[16,1,4096]{2,1,0:T(1,128)S(1)} async-done(((f32[16,1,4096]{2,1,0:T(1,128)}), f32[16,1,4096]{2,1,0:T(1,128)S(1)}, u32[]{:S(2)}, u32[]{:S(2)}) %all-to-all-start.5) | async-done | bytes 262176 | tf_op jit(solution)/shard_map/all_to_all | solution.py:11
  106.3 2.8 %multiply_reduce_fusion.6 = (f32[4]{0:T(128)S(1)}, f32[4]{0:T(128)S(1)}, f32[4]{0:T(128)S(1)}, f32[16,64,4]{1,2,0:T(4,128)S(1)}) fusion(f32[16,64,4]{1,2,0:T(4,128)S(1)} %broadcast_divide_fusion.1, f32[16,64,4]{1,2,0:T(4,128)S(1)} %subtract_divide_fusion.1, f32[16,576,4]{1,2,0:T(4,128)S(1)} %reshape.565, f32[16,64,576]{2,1,0:T(8,128)S(1)} %copy-done), kind=kOutput, calls=%fused_computation.28 | convolution fusion | flops 28336116 | bytes 2555952 | tf_op jit(solution)/shard_map/sac,scr->sar/dot_general | solution.py:73
  109.7 3.5 %all-to-all-start.6 = ((f32[16,1,4]{2,1,0:T(1,128)}), f32[16,1,4]{2,1,0:T(1,128)S(1)}, u32[]{:S(2)}, u32[]{:S(2)}) async-start(f32[16,1,4]{2,1,0:T(1,128)} %broadcast_in_dim.94), calls=%async_computation.6 | async-start | bytes 16384 | tf_op jit(solution)/shard_map/all_to_all | solution.py:11
  113.9 5.7 %all-to-all-done.6 = f32[16,1,4]{2,1,0:T(1,128)S(1)} async-done(((f32[16,1,4]{2,1,0:T(1,128)}), f32[16,1,4]{2,1,0:T(1,128)S(1)}, u32[]{:S(2)}, u32[]{:S(2)}) %all-to-all-start.6) | async-done | bytes 288 | tf_op jit(solution)/shard_map/all_to_all | solution.py:11
  120.1 3.5 %all-to-all-start.7 = ((f32[16,1,4]{2,1,0:T(1,128)}), f32[16,1,4]{2,1,0:T(1,128)S(1)}, u32[]{:S(2)}, u32[]{:S(2)}) async-start(f32[16,1,4]{2,1,0:T(1,128)} %broadcast_in_dim.95), calls=%async_computation.7 | async-start | bytes 16384 | tf_op jit(solution)/shard_map/all_to_all | solution.py:11
  124.3 5.6 %all-to-all-done.7 = f32[16,1,4]{2,1,0:T(1,128)S(1)} async-done(((f32[16,1,4]{2,1,0:T(1,128)}), f32[16,1,4]{2,1,0:T(1,128)S(1)}, u32[]{:S(2)}, u32[]{:S(2)}) %all-to-all-start.7) | async-done | bytes 288 | tf_op jit(solution)/shard_map/all_to_all | solution.py:11
  130.5 3.7 %all-to-all-start.8 = ((f32[16,1,4]{2,1,0:T(1,128)}), f32[16,1,4]{2,1,0:T(1,128)S(1)}, u32[]{:S(2)}, u32[]{:S(2)}) async-start(f32[16,1,4]{2,1,0:T(1,128)} %broadcast_in_dim.96), calls=%async_computation.8 | async-start | bytes 16384 | tf_op jit(solution)/shard_map/all_to_all | solution.py:11
  134.7 5.7 %all-to-all-done.8 = f32[16,1,4]{2,1,0:T(1,128)S(1)} async-done(((f32[16,1,4]{2,1,0:T(1,128)}), f32[16,1,4]{2,1,0:T(1,128)S(1)}, u32[]{:S(2)}, u32[]{:S(2)}) %all-to-all-start.8) | async-done | bytes 288 | tf_op jit(solution)/shard_map/all_to_all | solution.py:11
  142.2 3.5 %all-to-all-start.9 = ((f32[16,1,4096]{2,1,0:T(1,128)}), f32[16,1,4096]{2,1,0:T(1,128)S(1)}, u32[]{:S(2)}, u32[]{:S(2)}) async-start(f32[16,1,4096]{2,1,0:T(1,128)} %reshape.573), calls=%async_computation.9 | async-start | bytes 524288 | tf_op jit(solution)/shard_map/all_to_all | solution.py:11
  146.9 6.2 %all-to-all-done.9 = f32[16,1,4096]{2,1,0:T(1,128)S(1)} async-done(((f32[16,1,4096]{2,1,0:T(1,128)}), f32[16,1,4096]{2,1,0:T(1,128)S(1)}, u32[]{:S(2)}, u32[]{:S(2)}) %all-to-all-start.9) | async-done | bytes 262176 | tf_op jit(solution)/shard_map/all_to_all | solution.py:11
  155.3 2.8 %multiply_reduce_fusion = (f32[4]{0:T(128)S(1)}, f32[4]{0:T(128)S(1)}, f32[4]{0:T(128)S(1)}, f32[4]{0:T(128)S(1)}) fusion(f32[16,64,4]{1,2,0:T(4,128)S(1)} %subtract_divide_fusion, f32[16,64,4]{1,2,0:T(4,128)S(1)} %subtract_divide_fusion.1, f32[16,64,4]{1,2,0:T(4,128)S(1)} %broadcast_divide_fusion.1, f32[16,576,4]{1,2,0:T(4,128)S(1)} %reshape.566, ...), kind=kOutput, calls=%fused_computation.21 | convolution fusion | flops 28344304 | bytes 2555968 | tf_op jit(solution)/shard_map/sac,scr->sar/dot_general | solution.py:73
  158.7 3.5 %all-to-all-start.10 = ((f32[16,1,4]{2,1,0:T(1,128)}), f32[16,1,4]{2,1,0:T(1,128)S(1)}, u32[]{:S(2)}, u32[]{:S(2)}) async-start(f32[16,1,4]{2,1,0:T(1,128)} %broadcast_in_dim.99), calls=%async_computation.10 | async-start | bytes 16384 | tf_op jit(solution)/shard_map/all_to_all | solution.py:11
  162.2 6.2 %all-to-all-done.10 = f32[16,1,4]{2,1,0:T(1,128)S(1)} async-done(((f32[16,1,4]{2,1,0:T(1,128)}), f32[16,1,4]{2,1,0:T(1,128)S(1)}, u32[]{:S(2)}, u32[]{:S(2)}) %all-to-all-start.10) | async-done | bytes 288 | tf_op jit(solution)/shard_map/all_to_all | solution.py:11
  169.1 3.5 %all-to-all-start.11 = ((f32[16,1,4]{2,1,0:T(1,128)}), f32[16,1,4]{2,1,0:T(1,128)S(1)}, u32[]{:S(2)}, u32[]{:S(2)}) async-start(f32[16,1,4]{2,1,0:T(1,128)} %broadcast_in_dim.100), calls=%async_computation.11 | async-start | bytes 16384 | tf_op jit(solution)/shard_map/all_to_all | solution.py:11
  172.6 6.3 %all-to-all-done.11 = f32[16,1,4]{2,1,0:T(1,128)S(1)} async-done(((f32[16,1,4]{2,1,0:T(1,128)}), f32[16,1,4]{2,1,0:T(1,128)S(1)}, u32[]{:S(2)}, u32[]{:S(2)}) %all-to-all-start.11) | async-done | bytes 288 | tf_op jit(solution)/shard_map/all_to_all | solution.py:11
  179.4 3.5 %all-to-all-start.12 = ((f32[16,1,4]{2,1,0:T(1,128)}), f32[16,1,4]{2,1,0:T(1,128)S(1)}, u32[]{:S(2)}, u32[]{:S(2)}) async-start(f32[16,1,4]{2,1,0:T(1,128)} %broadcast_in_dim.101), calls=%async_computation.12 | async-start | bytes 16384 | tf_op jit(solution)/shard_map/all_to_all | solution.py:11
  184.4 4.9 %all-to-all-done.12 = f32[16,1,4]{2,1,0:T(1,128)S(1)} async-done(((f32[16,1,4]{2,1,0:T(1,128)}), f32[16,1,4]{2,1,0:T(1,128)S(1)}, u32[]{:S(2)}, u32[]{:S(2)}) %all-to-all-start.12) | async-done | bytes 288 | tf_op jit(solution)/shard_map/all_to_all | solution.py:11
  189.8 3.5 %all-to-all-start.13 = ((f32[16,1,4]{2,1,0:T(1,128)}), f32[16,1,4]{2,1,0:T(1,128)S(1)}, u32[]{:S(2)}, u32[]{:S(2)}) async-start(f32[16,1,4]{2,1,0:T(1,128)} %broadcast_in_dim.102), calls=%async_computation.13 | async-start | bytes 16384 | tf_op jit(solution)/shard_map/all_to_all | solution.py:11
  193.5 6.2 %all-to-all-done.13 = f32[16,1,4]{2,1,0:T(1,128)S(1)} async-done(((f32[16,1,4]{2,1,0:T(1,128)}), f32[16,1,4]{2,1,0:T(1,128)S(1)}, u32[]{:S(2)}, u32[]{:S(2)}) %all-to-all-start.13) | async-done | bytes 288 | tf_op jit(solution)/shard_map/all_to_all | solution.py:11
  199.6 1.8 fusion.28
  206.9 25.4 %all_to_all.112 = f32[16,1,256]{2,1,0:T(1,128)S(1)} all-to-all(f32[16,1,256]{2,1,0:T(1,128)S(1)} %reshape.575), channel_id=1, replica_groups=mesh['grp'=16,'sub'=16] {'grp'}, dimensions={0} | all-to-all | bytes 32768 | tf_op jit(solution)/shard_map/all_to_all | solution.py:95
  (148 shorter events, 36.7 us)
Async XLA Ops:
  6.5 60.6 %all-gather.2.cloned.1.call-start = ((), (), s32[]{:S(2)}) async-start(), calls=%async_computation.15 | async-start | bytes 2785280 | tf_op jit(solution)/shard_map/all_gather | solution.py:44
  10.1 17.3 %all-to-all-start = ((f32[16,1,256]{2,1,0:T(1,128)}), f32[16,1,256]{2,1,0:T(1,128)S(1)}, u32[]{:S(2)}, u32[]{:S(2)}) async-start(f32[16,1,256]{2,1,0:T(1,128)} %reshape.567), calls=%async_computation | async-start | bytes 32768 | tf_op jit(solution)/shard_map/all_to_all | solution.py:45
  29.0 20.6 %all-to-all-start.1 = ((f32[16,1,4]{2,1,0:T(1,128)}), f32[16,1,4]{2,1,0:T(1,128)S(1)}, u32[]{:S(2)}, u32[]{:S(2)}) async-start(f32[16,1,4]{2,1,0:T(1,128)} %broadcast_in_dim.48), calls=%async_computation.1 | async-start | bytes 16384 | tf_op jit(solution)/shard_map/all_to_all | solution.py:11
  50.8 14.1 %all-to-all-start.2 = ((f32[16,1,4096]{2,1,0:T(1,128)}), f32[16,1,4096]{2,1,0:T(1,128)S(1)}, u32[]{:S(2)}, u32[]{:S(2)}) async-start(f32[16,1,4096]{2,1,0:T(1,128)} %reshape.569), calls=%async_computation.2 | async-start | bytes 524288 | tf_op jit(solution)/shard_map/all_to_all | solution.py:11
  67.1 29.8 %copy-start.12 = (s32[3]{0:T(128)S(1)}, s32[3]{0:T(128)}, u32[]{:S(2)}) copy-start(s32[3]{0:T(128)} %constant.391.clone.1) | copy-start | bytes 40
  82.0 9.8 %all-to-all-start.4 = ((f32[16,1,4]{2,1,0:T(1,128)}), f32[16,1,4]{2,1,0:T(1,128)S(1)}, u32[]{:S(2)}, u32[]{:S(2)}) async-start(f32[16,1,4]{2,1,0:T(1,128)} %broadcast_in_dim.91), calls=%async_computation.4 | async-start | bytes 16384 | tf_op jit(solution)/shard_map/all_to_all | solution.py:11
  85.5 12.0 %copy-start.3 = (f32[4]{0:T(128)}, f32[4]{0:T(128)S(1)}, u32[]{:S(2)}) copy-start(f32[4]{0:T(128)S(1)} %reduce_sum.199) | copy-start | bytes 52
  91.8 5.7 %copy-start.9 = (f32[4]{0:T(128)}, f32[4]{0:T(128)S(1)}, u32[]{:S(2)}) copy-start(f32[4]{0:T(128)S(1)} %reduce_sum.201) | copy-start | bytes 52
  93.0 13.3 %copy-start = (f32[16,64,576]{2,1,0:T(8,128)S(1)}, f32[16,64,576]{2,1,0:T(8,128)}, u32[]{:S(2)}) copy-start(f32[16,64,576]{2,1,0:T(8,128)} %all-gather.2.cloned.1.call-done) | copy-start | bytes 7077892
  93.0 11.1 %all-to-all-start.5 = ((f32[16,1,4096]{2,1,0:T(1,128)}), f32[16,1,4096]{2,1,0:T(1,128)S(1)}, u32[]{:S(2)}, u32[]{:S(2)}) async-start(f32[16,1,4096]{2,1,0:T(1,128)} %reshape.571), calls=%async_computation.5 | async-start | bytes 524288 | tf_op jit(solution)/shard_map/all_to_all | solution.py:11
  106.3 40.0 %copy-start.4 = (f32[4]{0:T(128)S(1)}, f32[4]{0:T(128)}, u32[]{:S(2)}) copy-start(f32[4]{0:T(128)} %copy-done.3) | copy-start | bytes 52
  106.3 40.0 %copy-start.10 = (f32[4]{0:T(128)S(1)}, f32[4]{0:T(128)}, u32[]{:S(2)}) copy-start(f32[4]{0:T(128)} %copy-done.9) | copy-start | bytes 52
  109.7 9.8 %all-to-all-start.6 = ((f32[16,1,4]{2,1,0:T(1,128)}), f32[16,1,4]{2,1,0:T(1,128)S(1)}, u32[]{:S(2)}, u32[]{:S(2)}) async-start(f32[16,1,4]{2,1,0:T(1,128)} %broadcast_in_dim.94), calls=%async_computation.6 | async-start | bytes 16384 | tf_op jit(solution)/shard_map/all_to_all | solution.py:11
  120.1 9.8 %all-to-all-start.7 = ((f32[16,1,4]{2,1,0:T(1,128)}), f32[16,1,4]{2,1,0:T(1,128)S(1)}, u32[]{:S(2)}, u32[]{:S(2)}) async-start(f32[16,1,4]{2,1,0:T(1,128)} %broadcast_in_dim.95), calls=%async_computation.7 | async-start | bytes 16384 | tf_op jit(solution)/shard_map/all_to_all | solution.py:11
  130.5 10.0 %all-to-all-start.8 = ((f32[16,1,4]{2,1,0:T(1,128)}), f32[16,1,4]{2,1,0:T(1,128)S(1)}, u32[]{:S(2)}, u32[]{:S(2)}) async-start(f32[16,1,4]{2,1,0:T(1,128)} %broadcast_in_dim.96), calls=%async_computation.8 | async-start | bytes 16384 | tf_op jit(solution)/shard_map/all_to_all | solution.py:11
  134.7 12.2 %copy-start.1 = (f32[4]{0:T(128)}, f32[4]{0:T(128)S(1)}, u32[]{:S(2)}) copy-start(f32[4]{0:T(128)S(1)} %reduce_sum.204) | copy-start | bytes 52
  140.5 0.5 copy-start.6
  142.2 10.8 %all-to-all-start.9 = ((f32[16,1,4096]{2,1,0:T(1,128)}), f32[16,1,4096]{2,1,0:T(1,128)S(1)}, u32[]{:S(2)}, u32[]{:S(2)}) async-start(f32[16,1,4096]{2,1,0:T(1,128)} %reshape.573), calls=%async_computation.9 | async-start | bytes 524288 | tf_op jit(solution)/shard_map/all_to_all | solution.py:11
  154.6 7.5 %copy-start.5 = (f32[4]{0:T(128)S(1)}, f32[4]{0:T(128)}, u32[]{:S(2)}) copy-start(f32[4]{0:T(128)} %copy-done.3) | copy-start | bytes 52
  154.6 7.6 %copy-start.11 = (f32[1,1,4]{2,1,0:T(1,128)S(1)}, f32[1,1,4]{2,1,0:T(1,128)}, u32[]{:S(2)}) copy-start(f32[1,1,4]{2,1,0:T(1,128)} %fusion.27) | copy-start | bytes 52
  154.6 17.9 %copy-start.2 = (f32[4]{0:T(128)S(1)}, f32[4]{0:T(128)}, u32[]{:S(2)}) copy-start(f32[4]{0:T(128)} %copy-done.1) | copy-start | bytes 52
  154.6 17.9 %copy-start.7 = (f32[4]{0:T(128)S(1)}, f32[4]{0:T(128)}, u32[]{:S(2)}) copy-start(f32[4]{0:T(128)} %copy-done.6) | copy-start | bytes 52
  154.7 49.9 %copy-start.13 = (pred[3,3]{1,0:T(4,128)(4,1)S(1)}, pred[3,3]{1,0:T(4,128)(4,1)}, u32[]{:S(2)}) copy-start(pred[3,3]{1,0:T(4,128)(4,1)} %iota_compare_fusion.2) | copy-start | bytes 31
  154.7 50.1 %copy-start.8 = (pred[3,3]{1,0:T(4,128)(4,1)S(1)}, pred[3,3]{1,0:T(4,128)(4,1)}, u32[]{:S(2)}) copy-start(pred[3,3]{1,0:T(4,128)(4,1)} %iota_compare_fusion.3) | copy-start | bytes 31
  158.7 9.8 %all-to-all-start.10 = ((f32[16,1,4]{2,1,0:T(1,128)}), f32[16,1,4]{2,1,0:T(1,128)S(1)}, u32[]{:S(2)}, u32[]{:S(2)}) async-start(f32[16,1,4]{2,1,0:T(1,128)} %broadcast_in_dim.99), calls=%async_computation.10 | async-start | bytes 16384 | tf_op jit(solution)/shard_map/all_to_all | solution.py:11
  169.1 9.8 %all-to-all-start.11 = ((f32[16,1,4]{2,1,0:T(1,128)}), f32[16,1,4]{2,1,0:T(1,128)S(1)}, u32[]{:S(2)}, u32[]{:S(2)}) async-start(f32[16,1,4]{2,1,0:T(1,128)} %broadcast_in_dim.100), calls=%async_computation.11 | async-start | bytes 16384 | tf_op jit(solution)/shard_map/all_to_all | solution.py:11
  179.4 9.8 %all-to-all-start.12 = ((f32[16,1,4]{2,1,0:T(1,128)}), f32[16,1,4]{2,1,0:T(1,128)S(1)}, u32[]{:S(2)}, u32[]{:S(2)}) async-start(f32[16,1,4]{2,1,0:T(1,128)} %broadcast_in_dim.101), calls=%async_computation.12 | async-start | bytes 16384 | tf_op jit(solution)/shard_map/all_to_all | solution.py:11
  189.8 9.8 %all-to-all-start.13 = ((f32[16,1,4]{2,1,0:T(1,128)}), f32[16,1,4]{2,1,0:T(1,128)S(1)}, u32[]{:S(2)}, u32[]{:S(2)}) async-start(f32[16,1,4]{2,1,0:T(1,128)} %broadcast_in_dim.102), calls=%async_computation.13 | async-start | bytes 16384 | tf_op jit(solution)/shard_map/all_to_all | solution.py:11
Sparse Core Ops, SparseCore 0:
  9.2 44.2 all-gather.1
where the time goes:
time: 242 us; the launch traced here: 241 us
  waiting for transfers between devices  71.7 us (30%)
  starting transfers between devices  58.7 us (24%)
  blocking collectives  35.2 us (15%)
  local copies, waits for them, and re-layouts  34.1 us (14%)
  other arithmetic  15.4 us (6%)
  between operations  14 us (6%)
  matrix products  11.5 us (5%)
    all_to_all x12, waiting for transfers between devices, from_everyone(): return lax.all_to_all(copies, axis, split_axis=0, concat_axis=0, tiled=True)  66.9 us
    all_to_all x12, starting transfers between devices, from_everyone(): return lax.all_to_all(copies, axis, split_axis=0, concat_axis=0, tiled=True)  48.7 us
    all_to_all x1, blocking collectives, per_device(): lax.all_to_all(solution, 'grp', split_axis=0, concat_axis=2, tiled=True)  25.4 us
    gather x3, local copies, waits for them, and re-layouts, per_device(): link = inverse[neighbor_table[owner_map]]  14 us
    dot_general x3, matrix products, per_device(): jnp.einsum('sac,scr->sar', op_rows, stacked, precision=lax.Precision.HIGH...  10.1 us
    all_to_all x1, starting transfers between devices, per_device(): lax.all_to_all(right_side, 'grp', split_axis=2, concat_axis=0, tiled=True)  9.97 us
    all_to_all x1, blocking collectives, from_everyone(): return lax.all_to_all(copies, axis, split_axis=0, concat_axis=0, tiled=True)  9.8 us
    unnamed x48, local copies, waits for them, and re-layouts  7.99 us
  transfers between devices with their start and end apart: 14, of which 12 were waited for; matrix products, arithmetic and copies ran while one was open for 13% of the time, Pallas kernels for 0%

commit v1 on v0

--- a/solution.py
+++ b/solution.py
@@ -1,9 +1,30 @@
+import functools
 import jax
 import jax.numpy as jnp
 from jax import lax
 from jax.sharding import PartitionSpec as P
 
 ITERS = 3
+
+
+def build_corner_here(page, mesh_ax):
+    prior, part_next = (lax.axis_size(mesh_ax), lax.axis_index(mesh_ax))
+    local_out = page.shape[2] // prior
+    g_now = jnp.roll(page, -part_next * local_out, axis=2)
+    views = [lax.slice_in_dim(g_now, 0, local_out, axis=2)]
+    for dev_i in range(1, prior):
+        then = lax.slice_in_dim(g_now, dev_i * local_out, (dev_i + 1) * local_out, axis=2)
+        views.append(
+            lax.ppermute(
+                then, axis_name=mesh_ax, perm=[(kk, (kk + dev_i) % prior) for kk in range(prior)]
+            )
+        )
+    return jnp.roll(
+        jnp.concatenate(views[::-1], axis=0), (part_next + 1) * views[0].shape[0], axis=0
+    )
+
+
+work_leaves = functools.partial(build_corner_here, mesh_ax="grp")
 
 
 def from_everyone(array, axis):
@@ -42,7 +63,7 @@
     )
     link = inverse[neighbor_table[owner_map]]
     op_rows = lax.all_gather(coarse_op, "grp", axis=0, tiled=True)
-    rhs_rows = lax.all_to_all(right_side, "grp", split_axis=2, concat_axis=0, tiled=True)
+    rhs_rows = work_leaves(right_side)
 
     def reduce_sum(values):
         return jax.tree.map(lambda part: over_copies(part, "sub"), values)

time: 242 us -> 257 us (1.062)
  blocking collectives: 35.2 us -> 51.9 us
  starting transfers between devices: 58.7 us -> 72.2 us
  waiting for transfers between devices: 71.7 us -> 62.2 us
  other arithmetic: 15.4 us -> 11.7 us
    ppermute x0 -> x15, starting transfers between devices: none -> 30.2 us  [build_corner_here(): lax.ppermute(then, axis_name=mesh_ax, perm=[(kk, (kk + dev_i) % prior) fo...]
    all_to_all x1 -> x2, blocking collectives: 9.8 us -> 23 us  [from_everyone(): return lax.all_to_all(copies, axis, split_axis=0, concat_axis=0, tiled=True)]
    all_to_all x1 -> x0, starting transfers between devices: 9.97 us -> none  [per_device(): lax.all_to_all(right_side, 'grp', split_axis=2, concat_axis=0, tiled=True)]
    all_to_all x12 -> x11, waiting for transfers between devices: 66.9 us -> 60.1 us  [from_everyone(): return lax.all_to_all(copies, axis, split_axis=0, concat_axis=0, tiled=True)]
    all_to_all x12 -> x11, starting transfers between devices: 48.7 us -> 42 us  [from_everyone(): return lax.all_to_all(copies, axis, split_axis=0, concat_axis=0, tiled=True)]
    all_to_all x1 -> x0, waiting for transfers between devices: 4.13 us -> none  [per_device(): lax.all_to_all(right_side, 'grp', split_axis=2, concat_axis=0, tiled=True)]
    all_to_all x1, blocking collectives: 25.4 us -> 28.9 us  [per_device(): lax.all_to_all(solution, 'grp', split_axis=0, concat_axis=2, tiled=True)]
    unnamed x48 -> x60, local copies, waits for them, and re-layouts: 7.99 us -> 5.63 us
  transfers between devices with their start and end apart: 14 -> 27, of which waited for: 12 -> 13; matrix products, arithmetic and copies ran while one was open for 13% -> 10% of each run, Pallas kernels for 0% -> 0%
where the time goes in v1:
time: 257 us; the launch traced here: 256 us
  starting transfers between devices  72.2 us (28%)
  waiting for transfers between devices  62.2 us (24%)
  blocking collectives  51.9 us (20%)
  local copies, waits for them, and re-layouts  32.2 us (13%)
  between operations  14.1 us (5%)
  other arithmetic  11.7 us (5%)
  matrix products  11.5 us (4%)
    all_to_all x11, waiting for transfers between devices, from_everyone(): return lax.all_to_all(copies, axis, split_axis=0, concat_axis=0, tiled=True)  60.1 us
    all_to_all x11, starting transfers between devices, from_everyone(): return lax.all_to_all(copies, axis, split_axis=0, concat_axis=0, tiled=True)  42 us
    ppermute x15, starting transfers between devices, build_corner_here(): lax.ppermute(then, axis_name=mesh_ax, perm=[(kk, (kk + dev_i) % prior) fo...  30.2 us
    all_to_all x1, blocking collectives, per_device(): lax.all_to_all(solution, 'grp', split_axis=0, concat_axis=2, tiled=True)  28.9 us
    all_to_all x2, blocking collectives, from_everyone(): return lax.all_to_all(copies, axis, split_axis=0, concat_axis=0, tiled=True)  23 us
    gather x3, local copies, waits for them, and re-layouts, per_device(): link = inverse[neighbor_table[owner_map]]  14 us
    dot_general x3, matrix products, per_device(): jnp.einsum('sac,scr->sar', op_rows, stacked, precision=lax.Precision.HIGH...  10.1 us
    unnamed x60, local copies, waits for them, and re-layouts  5.63 us
  transfers between devices with their start and end apart: 27, of which 13 were waited for; matrix products, arithmetic and copies ran while one was open for 10% of the time, Pallas kernels for 0%

profile of v1, /device:TPU:1, one launch (start us, length us, event | category | flops | bytes accessed | tf_op | source)
XLA Modules:
  0.0 255.9 jit_solution(8377357582390930401)
XLA Ops:
  7.4 3.2 %collective-permute-start = (f32[1,64,4]{1,2,0:T(4,128)S(1)}, f32[1,64,4]{1,2,0:T(4,128)S(1)}, u32[]{:S(2)}, u32[]{:S(2)}) collective-permute-start(f32[1,64,4]{1,2,0:T(4,128)S(1)} %get-tuple-element.136), channel_id=1, source_target_pairs={{0,240},{16,0},{32,16},{48,32},{64,48},{80,64},{96,80},{112,96},{1... | collective-permute-start | bytes 3080 | tf_op jit(solution)/shard_map/ppermute | solution.py:18
  10.7 3.9 %collective-permute-start.1 = (f32[1,64,4]{1,2,0:T(4,128)S(1)}, f32[1,64,4]{1,2,0:T(4,128)S(1)}, u32[]{:S(2)}, u32[]{:S(2)}) collective-permute-start(f32[1,64,4]{1,2,0:T(4,128)S(1)} %get-tuple-element.135), channel_id=1, source_target_pairs={{0,224},{16,240},{32,0},{48,16},{64,32},{80,48},{96,64},{112,80},{... | collective-permute-start | bytes 3080 | tf_op jit(solution)/shard_map/ppermute | solution.py:18
  19.1 4.9 %collective-permute-start.5 = (f32[1,64,4]{1,2,0:T(4,128)S(1)}, f32[1,64,4]{1,2,0:T(4,128)S(1)}, u32[]{:S(2)}, u32[]{:S(2)}) collective-permute-start(f32[1,64,4]{1,2,0:T(4,128)S(1)} %get-tuple-element.131), channel_id=1, source_target_pairs={{0,160},{16,176},{32,192},{48,208},{64,224},{80,240},{96,0},{112,1... | collective-permute-start | bytes 3080 | tf_op jit(solution)/shard_map/ppermute | solution.py:18
  25.1 4.5 %collective-permute-start.7 = (f32[1,64,4]{1,2,0:T(4,128)S(1)}, f32[1,64,4]{1,2,0:T(4,128)S(1)}, u32[]{:S(2)}, u32[]{:S(2)}) collective-permute-start(f32[1,64,4]{1,2,0:T(4,128)S(1)} %get-tuple-element.129), channel_id=1, source_target_pairs={{0,128},{16,144},{32,160},{48,176},{64,192},{80,208},{96,224},{112... | collective-permute-start | bytes 3080 | tf_op jit(solution)/shard_map/ppermute | solution.py:18
  30.9 2.8 %collective-permute-start.9 = (f32[1,64,4]{1,2,0:T(4,128)S(1)}, f32[1,64,4]{1,2,0:T(4,128)S(1)}, u32[]{:S(2)}, u32[]{:S(2)}) collective-permute-start(f32[1,64,4]{1,2,0:T(4,128)S(1)} %get-tuple-element.127), channel_id=1, source_target_pairs={{0,96},{16,112},{32,128},{48,144},{64,160},{80,176},{96,192},{112,... | collective-permute-start | bytes 3080 | tf_op jit(solution)/shard_map/ppermute | solution.py:18
  43.3 6.8 %all-to-all-start = ((f32[16,1,4]{2,1,0:T(1,128)}), f32[16,1,4]{2,1,0:T(1,128)S(1)}, u32[]{:S(2)}, u32[]{:S(2)}) async-start(f32[16,1,4]{2,1,0:T(1,128)} %broadcast_in_dim.87), calls=%async_computation | async-start | bytes 16384 | tf_op jit(solution)/shard_map/all_to_all | solution.py:32
  50.1 6.4 %all-to-all-done = f32[16,1,4]{2,1,0:T(1,128)S(1)} async-done(((f32[16,1,4]{2,1,0:T(1,128)}), f32[16,1,4]{2,1,0:T(1,128)S(1)}, u32[]{:S(2)}, u32[]{:S(2)}) %all-to-all-start) | async-done | bytes 288 | tf_op jit(solution)/shard_map/all_to_all | solution.py:32
  57.7 3.7 %all-to-all-start.1 = ((f32[16,1,4096]{2,1,0:T(1,128)}), f32[16,1,4096]{2,1,0:T(1,128)S(1)}, u32[]{:S(2)}, u32[]{:S(2)}) async-start(f32[16,1,4096]{2,1,0:T(1,128)} %reshape.567), calls=%async_computation.1 | async-start | bytes 524288 | tf_op jit(solution)/shard_map/all_to_all | solution.py:32
  61.5 13.1 %gather_fusion.1 = s32[2048]{0:T(1024)S(1)} fusion(s32[256]{0:T(256)S(1)} %select_reduce_fusion, s32[2048]{0:T(1024)S(1)} %broadcast_clamp_fusion), kind=kCustom, calls=%fused_computation.1 | custom fusion | bytes 24576 | tf_op jit(solution)/shard_map/gather | solution.py:64
  78.0 4.5 %multiply_reduce_fusion.8 = (f32[4]{0:T(128)S(1)}, f32[4]{0:T(128)S(1)}, f32[16,64,4]{1,2,0:T(4,128)S(1)}) fusion(f32[16,64,4]{1,2,0:T(4,128)S(1)} %dynamic-slice_divide_fusion, f32[16,576,4]{1,2,0:T(4,128)S(1)} %reshape.564, f32[16,64,576]{2,1,0:T(8,128)} %all-gather.2.cloned.1.call-done), kind=kOutput, calls=%fused_computation.66 | convolution fusion | flops 28327928 | bytes 2539552 | tf_op jit(solution)/shard_map/sac,scr->sar/dot_general | solution.py:94
  82.6 12.7 %all_to_all.93 = f32[16,1,4]{2,1,0:T(1,128)S(1)} all-to-all(f32[16,1,4]{2,1,0:T(1,128)S(1)} %broadcast_in_dim.93), channel_id=1, replica_groups=mesh['grp'=16,'sub'=16] {'sub'}, dimensions={0} | all-to-all | bytes 512 | tf_op jit(solution)/shard_map/all_to_all | solution.py:32
  95.8 3.5 %all-to-all-start.3 = ((f32[16,1,4]{2,1,0:T(1,128)}), f32[16,1,4]{2,1,0:T(1,128)S(1)}, u32[]{:S(2)}, u32[]{:S(2)}) async-start(f32[16,1,4]{2,1,0:T(1,128)} %broadcast_in_dim.94), calls=%async_computation.3 | async-start | bytes 16384 | tf_op jit(solution)/shard_map/all_to_all | solution.py:32
  99.3 6.3 %all-to-all-done.3 = f32[16,1,4]{2,1,0:T(1,128)S(1)} async-done(((f32[16,1,4]{2,1,0:T(1,128)}), f32[16,1,4]{2,1,0:T(1,128)S(1)}, u32[]{:S(2)}, u32[]{:S(2)}) %all-to-all-start.3) | async-done | bytes 288 | tf_op jit(solution)/shard_map/all_to_all | solution.py:32
  106.2 10.3 %all_to_all.94 = f32[16,1,4096]{2,1,0:T(1,128)S(1)} all-to-all(f32[16,1,4096]{2,1,0:T(1,128)S(1)} %reshape.569), channel_id=1, replica_groups=mesh['grp'=16,'sub'=16] {'sub'}, dimensions={0} | all-to-all | bytes 524288 | tf_op jit(solution)/shard_map/all_to_all | solution.py:32
  122.0 3.5 %all-to-all-start.5 = ((f32[16,1,4]{2,1,0:T(1,128)}), f32[16,1,4]{2,1,0:T(1,128)S(1)}, u32[]{:S(2)}, u32[]{:S(2)}) async-start(f32[16,1,4]{2,1,0:T(1,128)} %broadcast_in_dim.97), calls=%async_computation.5 | async-start | bytes 16384 | tf_op jit(solution)/shard_map/all_to_all | solution.py:32
  126.2 5.6 %all-to-all-done.5 = f32[16,1,4]{2,1,0:T(1,128)S(1)} async-done(((f32[16,1,4]{2,1,0:T(1,128)}), f32[16,1,4]{2,1,0:T(1,128)S(1)}, u32[]{:S(2)}, u32[]{:S(2)}) %all-to-all-start.5) | async-done | bytes 288 | tf_op jit(solution)/shard_map/all_to_all | solution.py:32
  132.4 3.5 %all-to-all-start.6 = ((f32[16,1,4]{2,1,0:T(1,128)}), f32[16,1,4]{2,1,0:T(1,128)S(1)}, u32[]{:S(2)}, u32[]{:S(2)}) async-start(f32[16,1,4]{2,1,0:T(1,128)} %broadcast_in_dim.98), calls=%async_computation.6 | async-start | bytes 16384 | tf_op jit(solution)/shard_map/all_to_all | solution.py:32
  135.9 6.3 %all-to-all-done.6 = f32[16,1,4]{2,1,0:T(1,128)S(1)} async-done(((f32[16,1,4]{2,1,0:T(1,128)}), f32[16,1,4]{2,1,0:T(1,128)S(1)}, u32[]{:S(2)}, u32[]{:S(2)}) %all-to-all-start.6) | async-done | bytes 288 | tf_op jit(solution)/shard_map/all_to_all | solution.py:32
  142.8 3.5 %all-to-all-start.7 = ((f32[16,1,4]{2,1,0:T(1,128)}), f32[16,1,4]{2,1,0:T(1,128)S(1)}, u32[]{:S(2)}, u32[]{:S(2)}) async-start(f32[16,1,4]{2,1,0:T(1,128)} %broadcast_in_dim.99), calls=%async_computation.7 | async-start | bytes 16384 | tf_op jit(solution)/shard_map/all_to_all | solution.py:32
  146.4 6.2 %all-to-all-done.7 = f32[16,1,4]{2,1,0:T(1,128)S(1)} async-done(((f32[16,1,4]{2,1,0:T(1,128)}), f32[16,1,4]{2,1,0:T(1,128)S(1)}, u32[]{:S(2)}, u32[]{:S(2)}) %all-to-all-start.7) | async-done | bytes 288 | tf_op jit(solution)/shard_map/all_to_all | solution.py:32
  153.8 3.8 %all-to-all-start.8 = ((f32[16,1,4096]{2,1,0:T(1,128)}), f32[16,1,4096]{2,1,0:T(1,128)S(1)}, u32[]{:S(2)}, u32[]{:S(2)}) async-start(f32[16,1,4096]{2,1,0:T(1,128)} %reshape.571), calls=%async_computation.8 | async-start | bytes 524288 | tf_op jit(solution)/shard_map/all_to_all | solution.py:32
  159.0 5.6 %all-to-all-done.8 = f32[16,1,4096]{2,1,0:T(1,128)S(1)} async-done(((f32[16,1,4096]{2,1,0:T(1,128)}), f32[16,1,4096]{2,1,0:T(1,128)S(1)}, u32[]{:S(2)}, u32[]{:S(2)}) %all-to-all-start.8) | async-done | bytes 262176 | tf_op jit(solution)/shard_map/all_to_all | solution.py:32
  166.7 2.8 %multiply_reduce_fusion = (f32[4]{0:T(128)S(1)}, f32[4]{0:T(128)S(1)}, f32[4]{0:T(128)S(1)}, f32[4]{0:T(128)S(1)}) fusion(f32[16,64,4]{1,2,0:T(4,128)S(1)} %subtract_divide_fusion, f32[16,64,4]{1,2,0:T(4,128)S(1)} %subtract_divide_fusion.1, f32[16,64,4]{1,2,0:T(4,128)S(1)} %dynamic-slice_divide_fusion, f32[16,576,4]{1,2,0:T(4,128)S(1)} %reshape.566, ...), kind=kOutput, calls=%fused_computation.56 | convolution fusion | flops 28344304 | bytes 2555968 | tf_op jit(solution)/shard_map/sac,scr->sar/dot_general | solution.py:94
  170.2 3.5 %all-to-all-start.9 = ((f32[16,1,4]{2,1,0:T(1,128)}), f32[16,1,4]{2,1,0:T(1,128)S(1)}, u32[]{:S(2)}, u32[]{:S(2)}) async-start(f32[16,1,4]{2,1,0:T(1,128)} %broadcast_in_dim.102), calls=%async_computation.9 | async-start | bytes 16384 | tf_op jit(solution)/shard_map/all_to_all | solution.py:32
  173.7 6.2 %all-to-all-done.9 = f32[16,1,4]{2,1,0:T(1,128)S(1)} async-done(((f32[16,1,4]{2,1,0:T(1,128)}), f32[16,1,4]{2,1,0:T(1,128)S(1)}, u32[]{:S(2)}, u32[]{:S(2)}) %all-to-all-start.9) | async-done | bytes 288 | tf_op jit(solution)/shard_map/all_to_all | solution.py:32
  180.5 3.5 %all-to-all-start.10 = ((f32[16,1,4]{2,1,0:T(1,128)}), f32[16,1,4]{2,1,0:T(1,128)S(1)}, u32[]{:S(2)}, u32[]{:S(2)}) async-start(f32[16,1,4]{2,1,0:T(1,128)} %broadcast_in_dim.103), calls=%async_computation.10 | async-start | bytes 16384 | tf_op jit(solution)/shard_map/all_to_all | solution.py:32
  184.0 6.3 %all-to-all-done.10 = f32[16,1,4]{2,1,0:T(1,128)S(1)} async-done(((f32[16,1,4]{2,1,0:T(1,128)}), f32[16,1,4]{2,1,0:T(1,128)S(1)}, u32[]{:S(2)}, u32[]{:S(2)}) %all-to-all-start.10) | async-done | bytes 288 | tf_op jit(solution)/shard_map/all_to_all | solution.py:32
  190.9 3.5 %all-to-all-start.11 = ((f32[16,1,4]{2,1,0:T(1,128)}), f32[16,1,4]{2,1,0:T(1,128)S(1)}, u32[]{:S(2)}, u32[]{:S(2)}) async-start(f32[16,1,4]{2,1,0:T(1,128)} %broadcast_in_dim.104), calls=%async_computation.11 | async-start | bytes 16384 | tf_op jit(solution)/shard_map/all_to_all | solution.py:32
  195.7 5.0 %all-to-all-done.11 = f32[16,1,4]{2,1,0:T(1,128)S(1)} async-done(((f32[16,1,4]{2,1,0:T(1,128)}), f32[16,1,4]{2,1,0:T(1,128)S(1)}, u32[]{:S(2)}, u32[]{:S(2)}) %all-to-all-start.11) | async-done | bytes 288 | tf_op jit(solution)/shard_map/all_to_all | solution.py:32
  201.3 3.5 %all-to-all-start.12 = ((f32[16,1,4]{2,1,0:T(1,128)}), f32[16,1,4]{2,1,0:T(1,128)S(1)}, u32[]{:S(2)}, u32[]{:S(2)}) async-start(f32[16,1,4]{2,1,0:T(1,128)} %broadcast_in_dim.105), calls=%async_computation.12 | async-start | bytes 16384 | tf_op jit(solution)/shard_map/all_to_all | solution.py:32
  204.9 6.2 %all-to-all-done.12 = f32[16,1,4]{2,1,0:T(1,128)S(1)} async-done(((f32[16,1,4]{2,1,0:T(1,128)}), f32[16,1,4]{2,1,0:T(1,128)S(1)}, u32[]{:S(2)}, u32[]{:S(2)}) %all-to-all-start.12) | async-done | bytes 288 | tf_op jit(solution)/shard_map/all_to_all | solution.py:32
  218.7 28.9 %all_to_all.95 = f32[16,1,256]{2,1,0:T(1,128)S(1)} all-to-all(f32[16,1,256]{2,1,0:T(1,128)S(1)} %reshape.573), channel_id=1, replica_groups=mesh['grp'=16,'sub'=16] {'grp'}, dimensions={0} | all-to-all | bytes 32768 | tf_op jit(solution)/shard_map/all_to_all | solution.py:116
  (187 shorter events, 48.1 us)
Async XLA Ops:
  6.5 54.9 %copy-start.4 = (s32[256]{0:T(256)S(1)}, s32[256]{0:T(256)}, u32[]{:S(2)}) copy-start(s32[256]{0:T(256)} %param.24) | copy-start | bytes 3076
  6.5 71.5 %all-gather.2.cloned.1.call-start = ((), (), s32[]{:S(2)}) async-start(), calls=%async_computation.14 | async-start | bytes 2785280 | tf_op jit(solution)/shard_map/all_gather | solution.py:65
  7.4 11.7 %collective-permute-start = (f32[1,64,4]{1,2,0:T(4,128)S(1)}, f32[1,64,4]{1,2,0:T(4,128)S(1)}, u32[]{:S(2)}, u32[]{:S(2)}) collective-permute-start(f32[1,64,4]{1,2,0:T(4,128)S(1)} %get-tuple-element.136), channel_id=1, source_target_pairs={{0,240},{16,0},{32,16},{48,32},{64,48},{80,64},{96,80},{112,96},{1... | collective-permute-start | bytes 3080 | tf_op jit(solution)/shard_map/ppermute | solution.py:18
  10.7 13.4 %collective-permute-start.1 = (f32[1,64,4]{1,2,0:T(4,128)S(1)}, f32[1,64,4]{1,2,0:T(4,128)S(1)}, u32[]{:S(2)}, u32[]{:S(2)}) collective-permute-start(f32[1,64,4]{1,2,0:T(4,128)S(1)} %get-tuple-element.135), channel_id=1, source_target_pairs={{0,224},{16,240},{32,0},{48,16},{64,32},{80,48},{96,64},{112,80},{... | collective-permute-start | bytes 3080 | tf_op jit(solution)/shard_map/ppermute | solution.py:18
  14.5 10.6 %collective-permute-start.2 = (f32[1,64,4]{1,2,0:T(4,128)S(1)}, f32[1,64,4]{1,2,0:T(4,128)S(1)}, u32[]{:S(2)}, u32[]{:S(2)}) collective-permute-start(f32[1,64,4]{1,2,0:T(4,128)S(1)} %get-tuple-element.134), channel_id=1, source_target_pairs={{0,208},{16,224},{32,240},{48,0},{64,16},{80,32},{96,48},{112,64},... | collective-permute-start | bytes 3080 | tf_op jit(solution)/shard_map/ppermute | solution.py:18
  15.9 13.7 %collective-permute-start.3 = (f32[1,64,4]{1,2,0:T(4,128)S(1)}, f32[1,64,4]{1,2,0:T(4,128)S(1)}, u32[]{:S(2)}, u32[]{:S(2)}) collective-permute-start(f32[1,64,4]{1,2,0:T(4,128)S(1)} %get-tuple-element.133), channel_id=1, source_target_pairs={{0,192},{16,208},{32,224},{48,240},{64,0},{80,16},{96,32},{112,48}... | collective-permute-start | bytes 3080 | tf_op jit(solution)/shard_map/ppermute | solution.py:18
  16.7 14.2 %collective-permute-start.4 = (f32[1,64,4]{1,2,0:T(4,128)S(1)}, f32[1,64,4]{1,2,0:T(4,128)S(1)}, u32[]{:S(2)}, u32[]{:S(2)}) collective-permute-start(f32[1,64,4]{1,2,0:T(4,128)S(1)} %get-tuple-element.132), channel_id=1, source_target_pairs={{0,176},{16,192},{32,208},{48,224},{64,240},{80,0},{96,16},{112,32... | collective-permute-start | bytes 3080 | tf_op jit(solution)/shard_map/ppermute | solution.py:18
  19.1 14.6 %collective-permute-start.5 = (f32[1,64,4]{1,2,0:T(4,128)S(1)}, f32[1,64,4]{1,2,0:T(4,128)S(1)}, u32[]{:S(2)}, u32[]{:S(2)}) collective-permute-start(f32[1,64,4]{1,2,0:T(4,128)S(1)} %get-tuple-element.131), channel_id=1, source_target_pairs={{0,160},{16,176},{32,192},{48,208},{64,224},{80,240},{96,0},{112,1... | collective-permute-start | bytes 3080 | tf_op jit(solution)/shard_map/ppermute | solution.py:18
  24.0 12.3 %collective-permute-start.6 = (f32[1,64,4]{1,2,0:T(4,128)S(1)}, f32[1,64,4]{1,2,0:T(4,128)S(1)}, u32[]{:S(2)}, u32[]{:S(2)}) collective-permute-start(f32[1,64,4]{1,2,0:T(4,128)S(1)} %get-tuple-element.130), channel_id=1, source_target_pairs={{0,144},{16,160},{32,176},{48,192},{64,208},{80,224},{96,240},{112... | collective-permute-start | bytes 3080 | tf_op jit(solution)/shard_map/ppermute | solution.py:18
  25.1 11.2 %collective-permute-start.7 = (f32[1,64,4]{1,2,0:T(4,128)S(1)}, f32[1,64,4]{1,2,0:T(4,128)S(1)}, u32[]{:S(2)}, u32[]{:S(2)}) collective-permute-start(f32[1,64,4]{1,2,0:T(4,128)S(1)} %get-tuple-element.129), channel_id=1, source_target_pairs={{0,128},{16,144},{32,160},{48,176},{64,192},{80,208},{96,224},{112... | collective-permute-start | bytes 3080 | tf_op jit(solution)/shard_map/ppermute | solution.py:18
  29.6 8.7 %collective-permute-start.8 = (f32[1,64,4]{1,2,0:T(4,128)S(1)}, f32[1,64,4]{1,2,0:T(4,128)S(1)}, u32[]{:S(2)}, u32[]{:S(2)}) collective-permute-start(f32[1,64,4]{1,2,0:T(4,128)S(1)} %get-tuple-element.128), channel_id=1, source_target_pairs={{0,112},{16,128},{32,144},{48,160},{64,176},{80,192},{96,208},{112... | collective-permute-start | bytes 3080 | tf_op jit(solution)/shard_map/ppermute | solution.py:18
  30.9 8.9 %collective-permute-start.9 = (f32[1,64,4]{1,2,0:T(4,128)S(1)}, f32[1,64,4]{1,2,0:T(4,128)S(1)}, u32[]{:S(2)}, u32[]{:S(2)}) collective-permute-start(f32[1,64,4]{1,2,0:T(4,128)S(1)} %get-tuple-element.127), channel_id=1, source_target_pairs={{0,96},{16,112},{32,128},{48,144},{64,160},{80,176},{96,192},{112,... | collective-permute-start | bytes 3080 | tf_op jit(solution)/shard_map/ppermute | solution.py:18
  33.7 6.6 %collective-permute-start.10 = (f32[1,64,4]{1,2,0:T(4,128)S(1)}, f32[1,64,4]{1,2,0:T(4,128)S(1)}, u32[]{:S(2)}, u32[]{:S(2)}) collective-permute-start(f32[1,64,4]{1,2,0:T(4,128)S(1)} %get-tuple-element.126), channel_id=1, source_target_pairs={{0,80},{16,96},{32,112},{48,128},{64,144},{80,160},{96,176},{112,1... | collective-permute-start | bytes 3080 | tf_op jit(solution)/shard_map/ppermute | solution.py:18
  36.3 4.5 %collective-permute-start.11 = (f32[1,64,4]{1,2,0:T(4,128)S(1)}, f32[1,64,4]{1,2,0:T(4,128)S(1)}, u32[]{:S(2)}, u32[]{:S(2)}) collective-permute-start(f32[1,64,4]{1,2,0:T(4,128)S(1)} %get-tuple-element.125), channel_id=1, source_target_pairs={{0,64},{16,80},{32,96},{48,112},{64,128},{80,144},{96,160},{112,17... | collective-permute-start | bytes 3080 | tf_op jit(solution)/shard_map/ppermute | solution.py:18
  36.3 4.7 %collective-permute-start.12 = (f32[1,64,4]{1,2,0:T(4,128)S(1)}, f32[1,64,4]{1,2,0:T(4,128)S(1)}, u32[]{:S(2)}, u32[]{:S(2)}) collective-permute-start(f32[1,64,4]{1,2,0:T(4,128)S(1)} %get-tuple-element.124), channel_id=1, source_target_pairs={{0,48},{16,64},{32,80},{48,96},{64,112},{80,128},{96,144},{112,160... | collective-permute-start | bytes 3080 | tf_op jit(solution)/shard_map/ppermute | solution.py:18
  38.3 4.0 %collective-permute-start.13 = (f32[1,64,4]{1,2,0:T(4,128)S(1)}, f32[1,64,4]{1,2,0:T(4,128)S(1)}, u32[]{:S(2)}, u32[]{:S(2)}) collective-permute-start(f32[1,64,4]{1,2,0:T(4,128)S(1)} %get-tuple-element.123), channel_id=1, source_target_pairs={{0,32},{16,48},{32,64},{48,80},{64,96},{80,112},{96,128},{112,144}... | collective-permute-start | bytes 3080 | tf_op jit(solution)/shard_map/ppermute | solution.py:18
  39.8 2.6 %collective-permute-start.14 = (f32[1,64,4]{1,2,0:T(4,128)S(1)}, f32[1,64,4]{1,2,0:T(4,128)S(1)}, u32[]{:S(2)}, u32[]{:S(2)}) collective-permute-start(f32[1,64,4]{1,2,0:T(4,128)S(1)} %get-tuple-element.122), channel_id=1, source_target_pairs={{0,16},{16,32},{32,48},{48,64},{64,80},{80,96},{96,112},{112,128},... | collective-permute-start | bytes 3080 | tf_op jit(solution)/shard_map/ppermute | solution.py:18
  42.6 63.1 %copy-start.1 = (f32[32,64,4]{1,2,0:T(4,128)}, f32[32,64,4]{1,2,0:T(4,128)S(1)}, u32[]{:S(2)}) copy-start(f32[32,64,4]{1,2,0:T(4,128)S(1)} %constant_dynamic-update-slice_fusion) | copy-start | bytes 98308
  43.3 13.1 %all-to-all-start = ((f32[16,1,4]{2,1,0:T(1,128)}), f32[16,1,4]{2,1,0:T(1,128)S(1)}, u32[]{:S(2)}, u32[]{:S(2)}) async-start(f32[16,1,4]{2,1,0:T(1,128)} %broadcast_in_dim.87), calls=%async_computation | async-start | bytes 16384 | tf_op jit(solution)/shard_map/all_to_all | solution.py:32
  57.7 17.7 %all-to-all-start.1 = ((f32[16,1,4096]{2,1,0:T(1,128)}), f32[16,1,4096]{2,1,0:T(1,128)S(1)}, u32[]{:S(2)}, u32[]{:S(2)}) async-start(f32[16,1,4096]{2,1,0:T(1,128)} %reshape.567), calls=%async_computation.1 | async-start | bytes 524288 | tf_op jit(solution)/shard_map/all_to_all | solution.py:32
  95.8 9.8 %all-to-all-start.3 = ((f32[16,1,4]{2,1,0:T(1,128)}), f32[16,1,4]{2,1,0:T(1,128)S(1)}, u32[]{:S(2)}, u32[]{:S(2)}) async-start(f32[16,1,4]{2,1,0:T(1,128)} %broadcast_in_dim.94), calls=%async_computation.3 | async-start | bytes 16384 | tf_op jit(solution)/shard_map/all_to_all | solution.py:32
  118.0 34.6 %copy-start.2 = (f32[32,64,4]{1,2,0:T(4,128)S(1)}, f32[32,64,4]{1,2,0:T(4,128)}, u32[]{:S(2)}) copy-start(f32[32,64,4]{1,2,0:T(4,128)} %copy-done.1) | copy-start | bytes 98308
  118.6 39.6 %copy-start.5 = (s32[3]{0:T(128)S(1)}, s32[3]{0:T(128)}, u32[]{:S(2)}) copy-start(s32[3]{0:T(128)} %constant.430.clone.1) | copy-start | bytes 40
  122.0 9.8 %all-to-all-start.5 = ((f32[16,1,4]{2,1,0:T(1,128)}), f32[16,1,4]{2,1,0:T(1,128)S(1)}, u32[]{:S(2)}, u32[]{:S(2)}) async-start(f32[16,1,4]{2,1,0:T(1,128)} %broadcast_in_dim.97), calls=%async_computation.5 | async-start | bytes 16384 | tf_op jit(solution)/shard_map/all_to_all | solution.py:32
  132.4 9.8 %all-to-all-start.6 = ((f32[16,1,4]{2,1,0:T(1,128)}), f32[16,1,4]{2,1,0:T(1,128)S(1)}, u32[]{:S(2)}, u32[]{:S(2)}) async-start(f32[16,1,4]{2,1,0:T(1,128)} %broadcast_in_dim.98), calls=%async_computation.6 | async-start | bytes 16384 | tf_op jit(solution)/shard_map/all_to_all | solution.py:32
  142.8 9.8 %all-to-all-start.7 = ((f32[16,1,4]{2,1,0:T(1,128)}), f32[16,1,4]{2,1,0:T(1,128)S(1)}, u32[]{:S(2)}, u32[]{:S(2)}) async-start(f32[16,1,4]{2,1,0:T(1,128)} %broadcast_in_dim.99), calls=%async_computation.7 | async-start | bytes 16384 | tf_op jit(solution)/shard_map/all_to_all | solution.py:32
  153.8 10.8 %all-to-all-start.8 = ((f32[16,1,4096]{2,1,0:T(1,128)}), f32[16,1,4096]{2,1,0:T(1,128)S(1)}, u32[]{:S(2)}, u32[]{:S(2)}) async-start(f32[16,1,4096]{2,1,0:T(1,128)} %reshape.571), calls=%async_computation.8 | async-start | bytes 524288 | tf_op jit(solution)/shard_map/all_to_all | solution.py:32
  166.1 52.3 %copy-start.3 = (f32[32,64,4]{1,2,0:T(4,128)S(1)}, f32[32,64,4]{1,2,0:T(4,128)}, u32[]{:S(2)}) copy-start(f32[32,64,4]{1,2,0:T(4,128)} %copy-done.1) | copy-start | bytes 98308
  170.2 9.8 %all-to-all-start.9 = ((f32[16,1,4]{2,1,0:T(1,128)}), f32[16,1,4]{2,1,0:T(1,128)S(1)}, u32[]{:S(2)}, u32[]{:S(2)}) async-start(f32[16,1,4]{2,1,0:T(1,128)} %broadcast_in_dim.102), calls=%async_computation.9 | async-start | bytes 16384 | tf_op jit(solution)/shard_map/all_to_all | solution.py:32
  180.5 9.8 %all-to-all-start.10 = ((f32[16,1,4]{2,1,0:T(1,128)}), f32[16,1,4]{2,1,0:T(1,128)S(1)}, u32[]{:S(2)}, u32[]{:S(2)}) async-start(f32[16,1,4]{2,1,0:T(1,128)} %broadcast_in_dim.103), calls=%async_computation.10 | async-start | bytes 16384 | tf_op jit(solution)/shard_map/all_to_all | solution.py:32
  190.9 9.8 %all-to-all-start.11 = ((f32[16,1,4]{2,1,0:T(1,128)}), f32[16,1,4]{2,1,0:T(1,128)S(1)}, u32[]{:S(2)}, u32[]{:S(2)}) async-start(f32[16,1,4]{2,1,0:T(1,128)} %broadcast_in_dim.104), calls=%async_computation.11 | async-start | bytes 16384 | tf_op jit(solution)/shard_map/all_to_all | solution.py:32
  201.3 9.8 %all-to-all-start.12 = ((f32[16,1,4]{2,1,0:T(1,128)}), f32[16,1,4]{2,1,0:T(1,128)S(1)}, u32[]{:S(2)}, u32[]{:S(2)}) async-start(f32[16,1,4]{2,1,0:T(1,128)} %broadcast_in_dim.105), calls=%async_computation.12 | async-start | bytes 16384 | tf_op jit(solution)/shard_map/all_to_all | solution.py:32
  (1 other events, 12.5 us)
Sparse Core Ops, SparseCore 0:
  16.8 41.6 all-gather.1
